TPU v7x, 256 devices: a whole 4x4x8 slice. The times are simulated.
256 devices in a mesh: ctx: 64 (over z, x_hi, y), tp: 4 (over x_lo, core).
Axes of the slice: x: 4 (x_hi: 2, x_lo: 2; x = x_hi * 2 + x_lo), y: 4, z: 8, core: 2. Of those that a mesh axis runs over, the one named last changes fastest.
Arguments:
- queries: bfloat16 [32768, 4096], P('ctx', 'tp'), may hold values from -22 to 22
- keys: bfloat16 [32768, 512], P('ctx', 'tp'), may hold values from -22 to 22
- values: bfloat16 [32768, 512], P('ctx', 'tp'), may hold values from -36 to 36
- positions: int32 [3, 32768], P(None, 'ctx'), may hold values from 0 to 32767
- segment_ids: int32 [32768], replicated, may hold values from 0 to 31, never falling along the last dimension, each value on 1 to 2048 neighbouring positions
- out_weight: bfloat16 [4096, 8192], P('tp', 'ctx'), may hold values from -0.09375 to 0.09375
- residual: bfloat16 [32768, 8192], P(('ctx', 'tp')), may hold values from -3 to 3
Outputs:
- layer_out: bfloat16 [32768, 8192], P(('ctx', 'tp'))
Inputs may be any that keep to these rules, and one draw needn't show every extreme that they name: `segment_ids`: ids never fall along the sequence; each document has 1 to 2048 tokens, and one has exactly 2048.
All inputs are finite; a program needn't handle non-finite values.
Results may differ from a plain program's by a relative error of at most 0.013.
Values may be sent and summed in bfloat16 or wider, within the bound.
A program may use at most 128 MiB of HBM per device.

v0:
```python
import math
import jax
import jax.numpy as jnp
from jax import lax
from jax.sharding import PartitionSpec as P

HD = 128
DOC = 2048
theta_base = 1000000.0


def from_behind(block, axis, distance):
    devices = range(lax.axis_size(axis))
    route = [(i - distance, i) for i in devices if i - distance in devices]
    return lax.ppermute(block, axis, route)


def rotary_tables(positions):
    half_dim = HD // 2
    freq_index = jnp.arange(half_dim)
    inv_freq = theta_base ** (-2.0 * freq_index.astype(jnp.float32) / HD)
    first_end = HD // 8
    second_end = first_end + 3 * HD // 16
    place = positions.astype(jnp.float32)
    chosen = jnp.where(
        freq_index[None, :] < first_end,
        place[0][:, None],
        jnp.where(freq_index[None, :] < second_end, place[1][:, None], place[2][:, None]),
    )
    angle = chosen * inv_freq[None, :]
    return (jnp.cos(angle), jnp.sin(angle))


def rotate(vectors, cosine_table, sine_table):
    half_dim = HD // 2
    lower_half = vectors[..., :half_dim]
    upper_half = vectors[..., half_dim:]
    cos_b = cosine_table[:, None, :]
    sin_b = sine_table[:, None, :]
    return jnp.concatenate(
        [lower_half * cos_b - upper_half * sin_b, upper_half * cos_b + lower_half * sin_b], axis=-1
    )


def on_device(queries, keys, values, positions, segment_ids, out_weight, residual):
    tok_rows = queries.shape[0]
    local_heads = queries.shape[1] // HD
    local_kv = keys.shape[1] // HD
    group_size = local_heads // local_kv
    reach_blocks = (DOC + tok_rows - 2) // tok_rows
    my_start = lax.axis_index("ctx") * tok_rows
    cosine_table, sine_table = rotary_tables(positions)
    rot_q = rotate(
        queries.reshape(tok_rows, local_heads, HD).astype(jnp.float32), cosine_table, sine_table
    ).astype(jnp.bfloat16)
    grouped = rot_q.reshape(tok_rows, local_kv, group_size, HD).transpose(1, 2, 0, 3)
    rot_k = rotate(
        keys.reshape(tok_rows, local_kv, HD).astype(jnp.float32), cosine_table, sine_table
    ).astype(jnp.bfloat16)
    key_flat = rot_k.reshape(tok_rows, local_kv * HD)
    query_index = my_start + jnp.arange(tok_rows, dtype=jnp.int32)
    query_seg = lax.dynamic_slice_in_dim(segment_ids, my_start, tok_rows, 0)
    score_scale = 1.0 / math.sqrt(HD)
    block_rows = math.gcd(tok_rows, 512)
    block_count = tok_rows // block_rows

    def absorb(running, stacked, offset):
        key_blocks = stacked[0].reshape(block_count, block_rows, local_kv, HD)
        value_blocks = stacked[1].reshape(block_count, block_rows, local_kv, HD)

        def advance(block_index, carried):
            key_block = lax.dynamic_index_in_dim(key_blocks, block_index, 0, keepdims=False)
            value_block = lax.dynamic_index_in_dim(value_blocks, block_index, 0, keepdims=False)
            key_first = offset + block_index * block_rows
            key_index = key_first + jnp.arange(block_rows, dtype=jnp.int32)
            key_seg = lax.dynamic_slice_in_dim(
                segment_ids, jnp.maximum(key_first, 0), block_rows, 0
            )
            allowed = (
                (key_index[None, :] <= query_index[:, None])
                & (key_index[None, :] >= 0)
                & (key_seg[None, :] == query_seg[:, None])
            )

            def update(current):
                row_peak, row_sum, weighted = current
                score = (
                    jnp.einsum(
                        "kgtd,nkd->kgtn", grouped, key_block, preferred_element_type=jnp.float32
                    )
                    * score_scale
                )
                score = jnp.where(allowed, score, -1e30)
                new_peak = jnp.maximum(row_peak, jnp.max(score, axis=-1))
                prob = jnp.where(allowed, jnp.exp(score - new_peak[..., None]), 0.0)
                rescale = jnp.exp(row_peak - new_peak)
                row_sum = row_sum * rescale + jnp.sum(prob, axis=-1)
                weighted = weighted * rescale[..., None] + jnp.einsum(
                    "kgtn,nkd->kgtd",
                    prob.astype(jnp.bfloat16),
                    value_block,
                    preferred_element_type=jnp.float32,
                )
                return (new_peak, row_sum, weighted)

            def keep_state(current):
                return current

            return lax.cond(jnp.any(allowed), update, keep_state, carried)

        return lax.fori_loop(0, block_count, advance, running)

    initial = (
        jnp.full((local_kv, group_size, tok_rows), -1e30, jnp.float32),
        jnp.zeros((local_kv, group_size, tok_rows), jnp.float32),
        jnp.zeros((local_kv, group_size, tok_rows, HD), jnp.float32),
    )
    own_pair = jnp.stack([key_flat, values], axis=0)
    state = absorb(initial, own_pair, my_start)

    def next_block(step_index, carried):
        moving, running = carried
        moving = from_behind(moving, "ctx", 1)
        running = absorb(running, moving, my_start - step_index * tok_rows)
        return (moving, running)

    moving, state = lax.fori_loop(1, reach_blocks + 1, next_block, (own_pair, state))
    row_peak, row_sum, weighted = state
    attended = (
        (weighted / row_sum[..., None])
        .transpose(2, 0, 1, 3)
        .reshape(tok_rows, local_heads * HD)
        .astype(jnp.bfloat16)
    )
    partial_sum = jnp.dot(
        attended,
        lax.all_gather(out_weight, "ctx", axis=1, tiled=True),
        preferred_element_type=jnp.float32,
    )
    partial_sum = partial_sum.astype(jnp.bfloat16).astype(jnp.float32)
    shared = lax.psum_scatter(
        partial_sum.astype(jnp.bfloat16), "tp", scatter_dimension=0, tiled=True
    ).astype(jnp.float32)
    return (shared + residual.astype(jnp.float32)).astype(jnp.bfloat16)


def solution(mesh):
    return jax.shard_map(
        on_device,
        mesh=mesh,
        in_specs=(
            P("ctx", "tp"),
            P("ctx", "tp"),
            P("ctx", "tp"),
            P(None, "ctx"),
            P(),
            P("tp", "ctx"),
            P(("ctx", "tp"), None),
        ),
        out_specs=P(("ctx", "tp"), None),
        check_vma=False,
    )
```

profile of v0, /device:TPU:1, one launch (start us, length us, event | category | flops | bytes accessed | tf_op | source)
XLA Modules:
  0.0 394.7 jit_solution(13520080402836505690)
XLA Ops:
  6.5 0.0 all-gather.2.cloned.1.call-start
  6.5 0.7 all-gather.2.cloned.1.call-update
  7.3 0.0 reduce-scatter.2.cloned.1.call-start
  7.3 0.7 convert_element_type.93
  8.0 1.5 copy.12
  9.5 0.3 convert.25
  9.8 0.8 fusion.44
  10.7 1.0 fusion.43
  12.3 0.0 copy-start.12
  12.4 0.0 copy-start.13
  12.4 0.0 copy-start.14
  12.4 0.0 copy-start.11
  12.4 0.0 copy-start.9
  12.4 0.0 copy-start.10
  12.4 0.6 fusion.41
  13.0 0.0 copy-done.7
  13.0 0.0 copy-done.12
  13.0 0.0 copy-done.13
  13.0 0.0 copy-done.14
  13.0 0.0 copy-done.11
  13.0 0.3 fusion.36
  13.4 0.1 maximum_bitcast_fusion
  13.5 0.7 copy.14
  14.1 0.0 copy-done.9
  14.2 0.0 copy-done.10
  14.2 1.5 broadcast_in_dim.135
  15.7 0.0 copy-done.5
  15.7 2.2 subtract_convert_fusion.1
  17.9 0.1 pad_maximum_fusion.1
  18.0 0.0 copy-start.8
  18.0 8.1 %conditional.2 = ((f32[1,8,512]{2,1,0:T(8,128)S(1)}, f32[1,8,512]{2,1,0:T(8,128)S(1)}, f32[1,8,512,128]{3,2,1,0:T(8,128)})) conditional(s32[]{:T(128)} %convert_element_type.95, (f32[1,8,512]{2,1,0:T(8,128)S(1)}, f32[1,8,512]{2,1,0:T(8,128)S(1)}, f32[1,8,512,128]{3,2,1,0:T(8,128)}) %tuple.39, (pred[512,512]{0,1:T(8,128)(4,1)S(1)}, ...), branch_computations={%region_1.2_spmd, %region_2.0_spmd} | conditional | flops 1102065664 | bytes 49021044 | solution.py:109
  18.0 0.0 copy-start
  18.0 0.0 copy-start.6
  18.0 1.5 fusion.2
  19.6 2.0 fusion.4
  21.6 0.0 copy-done
  21.6 3.1 bitcast_add_fusion
  24.8 0.0 copy-start.1
  24.8 1.3 copy-done.1
  26.1 1.0 pad_maximum_fusion
  27.1 47.2 %while.28 = (s32[]{:T(128)}, bf16[2,512,128]{2,1,0:T(8,128)(2,1)S(1)}, f32[1,8,512]{2,1,0:T(8,128)S(1)}, f32[1,8,512]{2,1,0:T(8,128)S(1)}, f32[1,8,512,128]{3,2,...) while((s32[]{:T(128)}, ...), condition=%wide.region_11.12_spmd.clone.clone, body=%wide.region_5.11_spmd.clone.clone.sunk | while | flops 1103378432 | bytes 50349432 | solution.py:127
  27.2 4.0 %collective-permute-start = (bf16[2,512,128]{2,1,0:T(8,128)(2,1)S(1)}, bf16[2,512,128]{2,1,0:T(8,128)(2,1)S(1)}, u32[]{:S(2)}, u32[]{:S(2)}) collective-permute-start(bf16[2,512,128]{2,1,0:T(8,128)(2,1)S(1)} %get-tuple-element.546), channel_id=1, source_target_pairs={{0,4},{4,8},{8,12},{12,16},{16,20},{20,24},{24,28},{28,32},{32,36}... | collective-permute-start | bytes 786440 | tf_op jit(solution)/shard_map/while/body/eval_jaxpr/ppermute | solution.py:15
  31.3 0.8 dynamic_slice.35
  32.0 1.1 fusion.49
  33.8 2.9 collective-permute-done
  36.7 11.1 %collective-permute-start = (bf16[2,512,128]{2,1,0:T(8,128)(2,1)S(1)}, bf16[2,512,128]{2,1,0:T(8,128)(2,1)S(1)}, u32[]{:S(2)}, u32[]{:S(2)}) collective-permute-start(bf16[2,512,128]{2,1,0:T(8,128)(2,1)S(1)} %get-tuple-element.546), channel_id=1, source_target_pairs={{0,4},{4,8},{8,12},{12,16},{16,20},{20,24},{24,28},{28,32},{32,36}... | collective-permute-start | bytes 786440 | tf_op jit(solution)/shard_map/while/body/eval_jaxpr/ppermute | solution.py:15
  47.8 0.8 dynamic_slice.35
  48.6 1.1 fusion.49
  50.4 0.7 collective-permute-done
  51.1 3.8 collective-permute-start
  55.0 0.8 dynamic_slice.35
  55.8 1.1 fusion.49
  57.5 0.7 collective-permute-done
  58.3 12.8 %collective-permute-start = (bf16[2,512,128]{2,1,0:T(8,128)(2,1)S(1)}, bf16[2,512,128]{2,1,0:T(8,128)(2,1)S(1)}, u32[]{:S(2)}, u32[]{:S(2)}) collective-permute-start(bf16[2,512,128]{2,1,0:T(8,128)(2,1)S(1)} %get-tuple-element.546), channel_id=1, source_target_pairs={{0,4},{4,8},{8,12},{12,16},{16,20},{20,24},{24,28},{28,32},{32,36}... | collective-permute-start | bytes 786440 | tf_op jit(solution)/shard_map/while/body/eval_jaxpr/ppermute | solution.py:15
  71.1 0.8 dynamic_slice.35
  71.9 1.1 fusion.49
  73.7 0.7 collective-permute-done
  74.4 1.9 copy.15
  76.3 0.3 divide_convert_fusion
  76.6 209.5 %all-gather.2.cloned.1.call-done = bf16[1024,8192]{1,0:T(8,128)(2,1)} async-done(((bf16[1024,128]{1,0:T(8,128)(2,1)}), bf16[1024,8192]{1,0:T(8,128)(2,1)}) %all-gather.2.cloned.1.call-update) | async-done | bytes 16777232 | tf_op jit(solution)/shard_map/all_gather | solution.py:137
  286.1 16.9 %convolution_convert_fusion = bf16[512,8192]{1,0:T(8,128)(2,1)} fusion(bf16[512,1024]{0,1:T(8,128)(2,1)S(1)} %bitcast.79, bf16[1024,8192]{1,0:T(8,128)(2,1)} %all-gather.2.cloned.1.call-done), kind=kOutput, calls=%fused_computation.45 | convolution fusion | flops 8594128896 | bytes 26214400 | tf_op jit(solution)/shard_map/dot_general | solution.py:135
  303.1 0.0 reduce-scatter.2.cloned.1.call-update
  303.1 81.3 %reduce-scatter.2.cloned.1.call-done = bf16[128,8192]{1,0:T(8,128)(2,1)} async-done(((bf16[512,8192]{1,0:T(8,128)(2,1)}), bf16[128,8192]{1,0:T(8,128)(2,1)}) %reduce-scatter.2.cloned.1.call-update) | async-done | bytes 2097168 | tf_op jit(solution)/shard_map/reduce_scatter | solution.py:141
  384.4 3.4 add_convert_fusion
  (36 shorter events, 0.2 us)
Async XLA Ops:
  6.5 9.1 %copy-start.5 = (bf16[512,128]{1,0:T(8,128)(2,1)S(1)}, bf16[512,128]{1,0:T(8,128)(2,1)}, u32[]{:S(2)}) copy-start(bf16[512,128]{1,0:T(8,128)(2,1)} %param.14) | copy-start | bytes 393220
  6.5 279.6 %all-gather.2.cloned.1.call-start = ((), (), s32[]{:S(2)}) async-start(), calls=%async_computation.1 | async-start | bytes 17039360 | tf_op jit(solution)/shard_map/all_gather | solution.py:137
  7.3 377.1 %reduce-scatter.2.cloned.1.call-start = ((), (), s32[]{:S(2)}) async-start(), calls=%async_computation.2 | async-start | bytes 10485760 | tf_op jit(solution)/shard_map/reduce_scatter | solution.py:141
  10.7 2.3 copy-start.7
  12.3 0.7 copy-start.12
  12.4 0.7 copy-start.13
  12.4 0.7 copy-start.14
  12.4 0.6 copy-start.11
  12.4 1.7 copy-start.9
  12.4 1.7 copy-start.10
  18.0 9.2 %copy-start.8 = (s32[512]{0:T(512)S(1)}, s32[512]{0:T(512)}, u32[]{:S(2)}) copy-start(s32[512]{0:T(512)} %copy-done.7) | copy-start | bytes 6148
  18.0 3.6 copy-start
  18.0 3.6 copy-start.6
  24.8 1.3 copy-start.1
  27.2 9.5 %collective-permute-start = (bf16[2,512,128]{2,1,0:T(8,128)(2,1)S(1)}, bf16[2,512,128]{2,1,0:T(8,128)(2,1)S(1)}, u32[]{:S(2)}, u32[]{:S(2)}) collective-permute-start(bf16[2,512,128]{2,1,0:T(8,128)(2,1)S(1)} %get-tuple-element.546), channel_id=1, source_target_pairs={{0,4},{4,8},{8,12},{12,16},{16,20},{20,24},{24,28},{28,32},{32,36}... | collective-permute-start | bytes 786440 | tf_op jit(solution)/shard_map/while/body/eval_jaxpr/ppermute | solution.py:15
  36.7 14.3 %collective-permute-start = (bf16[2,512,128]{2,1,0:T(8,128)(2,1)S(1)}, bf16[2,512,128]{2,1,0:T(8,128)(2,1)S(1)}, u32[]{:S(2)}, u32[]{:S(2)}) collective-permute-start(bf16[2,512,128]{2,1,0:T(8,128)(2,1)S(1)} %get-tuple-element.546), channel_id=1, source_target_pairs={{0,4},{4,8},{8,12},{12,16},{16,20},{20,24},{24,28},{28,32},{32,36}... | collective-permute-start | bytes 786440 | tf_op jit(solution)/shard_map/while/body/eval_jaxpr/ppermute | solution.py:15
  51.1 7.1 %collective-permute-start = (bf16[2,512,128]{2,1,0:T(8,128)(2,1)S(1)}, bf16[2,512,128]{2,1,0:T(8,128)(2,1)S(1)}, u32[]{:S(2)}, u32[]{:S(2)}) collective-permute-start(bf16[2,512,128]{2,1,0:T(8,128)(2,1)S(1)} %get-tuple-element.546), channel_id=1, source_target_pairs={{0,4},{4,8},{8,12},{12,16},{16,20},{20,24},{24,28},{28,32},{32,36}... | collective-permute-start | bytes 786440 | tf_op jit(solution)/shard_map/while/body/eval_jaxpr/ppermute | solution.py:15
  58.3 16.1 %collective-permute-start = (bf16[2,512,128]{2,1,0:T(8,128)(2,1)S(1)}, bf16[2,512,128]{2,1,0:T(8,128)(2,1)S(1)}, u32[]{:S(2)}, u32[]{:S(2)}) collective-permute-start(bf16[2,512,128]{2,1,0:T(8,128)(2,1)S(1)} %get-tuple-element.546), channel_id=1, source_target_pairs={{0,4},{4,8},{8,12},{12,16},{16,20},{20,24},{24,28},{28,32},{32,36}... | collective-permute-start | bytes 786440 | tf_op jit(solution)/shard_map/while/body/eval_jaxpr/ppermute | solution.py:15
  303.1 81.4 %copy-start.4 = (bf16[128,8192]{1,0:T(8,128)(2,1)S(1)}, bf16[128,8192]{1,0:T(8,128)(2,1)}, u32[]{:S(2)}) copy-start(bf16[128,8192]{1,0:T(8,128)(2,1)} %param.19) | copy-start | bytes 6291460
Sparse Core Ops, SparseCore 0:
  10.7 275.3 all-gather.1
  303.2 81.1 reduce-scatter.1
where the time goes:
time: 395 us
  waiting for transfers between devices  296 us (75%)
  starting transfers between devices  31.8 us (8%)
  matrix products  21.6 us (5%)
  other arithmetic  17.3 us (4%)
  between operations  14.3 us (4%)
  local copies, waits for them, and re-layouts  10.1 us (3%)
    all_gather x1, waiting for transfers between devices, on_device(): lax.all_gather(out_weight, 'ctx', axis=1, tiled=True)  209 us
    reduce_scatter x1, waiting for transfers between devices, on_device(): lax.psum_scatter(partial_sum.astype(jnp.bfloat16), 'tp', scatter_dimensio...  81.3 us
    ppermute x4, starting transfers between devices, from_behind(): return lax.ppermute(block, axis, route)  31.7 us
    dot_general x1, matrix products, on_device(): jnp.dot(attended, lax.all_gather(out_weight, 'ctx', axis=1, tiled=True),...  16.9 us
  transfers between devices with their start and end apart: 6, of which 6 were waited for; matrix products, arithmetic and copies ran while one was open for 7% of the time, Pallas kernels for 0%

commit v1 on v0

--- a/solution.py
+++ b/solution.py
@@ -134,7 +134,9 @@
     )
     partial_sum = jnp.dot(
         attended,
-        lax.all_gather(out_weight, "ctx", axis=1, tiled=True),
+        jnp.concatenate(
+            lax.all_to_all(jnp.stack([out_weight] * lax.axis_size("ctx")), "ctx", 0, 0), axis=1
+        ),
         preferred_element_type=jnp.float32,
     )
     partial_sum = partial_sum.astype(jnp.bfloat16).astype(jnp.float32)

time: 395 us -> 596 us (1.51)
  waiting for transfers between devices: 296 us -> 468 us
  starting transfers between devices: 31.8 us -> 45.8 us
  matrix products: 21.6 us -> 34.4 us
    all_to_all x0 -> x1, waiting for transfers between devices: none -> 253 us  [on_device(): lax.all_to_all(jnp.stack([out_weight] * lax.axis_size('ctx')), 'ctx', 0, 0)]
    all_gather x1 -> x0, waiting for transfers between devices: 209 us -> none  [on_device(): lax.all_gather(out_weight, 'ctx', axis=1, tiled=True)]
    reduce_scatter x1, waiting for transfers between devices: 81.3 us -> 152 us  [on_device(): lax.psum_scatter(partial_sum.astype(jnp.bfloat16), 'tp', scatter_dimensio...]
    ppermute x4, waiting for transfers between devices: 4.86 us -> 63 us  [from_behind(): return lax.ppermute(block, axis, route)]
    all_to_all x0 -> x1, starting transfers between devices: none -> 15.5 us  [on_device(): lax.all_to_all(jnp.stack([out_weight] * lax.axis_size('ctx')), 'ctx', 0, 0)]
    dot_general x1, matrix products: 16.9 us -> 29.8 us  [on_device(): jnp.dot(attended, jnp.concatenate(lax.all_to_all(jnp.stack([out_weight] *...]
    another operation x0 -> x1, local copies, waits for them, and re-layouts: none -> 5.97 us  [on_device(): jnp.stack([out_weight] * lax.axis_size('ctx'))]
  transfers between devices with their start and end apart: 6 -> 6, of which waited for: 6 -> 6; matrix products, arithmetic and copies ran while one was open for 7% -> 4% of each run, Pallas kernels for 0% -> 0%
where the time goes in v1:
time: 596 us
  waiting for transfers between devices  468 us (79%)
  starting transfers between devices  45.8 us (8%)
  matrix products  34.4 us (6%)
  local copies, waits for them, and re-layouts  14.9 us (2%)
  other arithmetic  14.9 us (2%)
  between operations  14.3 us (2%)
    all_to_all x1, waiting for transfers between devices, on_device(): lax.all_to_all(jnp.stack([out_weight] * lax.axis_size('ctx')), 'ctx', 0, 0)  253 us
    reduce_scatter x1, waiting for transfers between devices, on_device(): lax.psum_scatter(partial_sum.astype(jnp.bfloat16), 'tp', scatter_dimensio...  152 us
    ppermute x4, waiting for transfers between devices, from_behind(): return lax.ppermute(block, axis, route)  63 us
    ppermute x4, starting transfers between devices, from_behind(): return lax.ppermute(block, axis, route)  30.3 us
    dot_general x1, matrix products, on_device(): jnp.dot(attended, jnp.concatenate(lax.all_to_all(jnp.stack([out_weight] *...  29.8 us
    all_to_all x1, starting transfers between devices, on_device(): lax.all_to_all(jnp.stack([out_weight] * lax.axis_size('ctx')), 'ctx', 0, 0)  15.5 us
  transfers between devices with their start and end apart: 6, of which 6 were waited for; matrix products, arithmetic and copies ran while one was open for 4% of the time, Pallas kernels for 0%

profile of v1, /device:TPU:1, one launch (start us, length us, event | category | flops | bytes accessed | tf_op | source)
XLA Modules:
  0.0 595.8 jit_solution(15161622666981778575)
XLA Ops:
  6.5 1.1 copy.16
  7.6 6.0 %stack.8 = bf16[64,1024,128]{1,2,0:T(8,128)(2,1)} broadcast(bf16[1024,128]{0,1:T(8,128)(2,1)S(1)} %copy.16), dimensions={1,2} | broadcast | bytes 17039360 | tf_op jit(solution)/shard_map/stack | solution.py:138
  13.6 0.0 copy-start.8
  13.6 0.0 copy-start.5
  13.6 15.5 %all-to-all-start = ((bf16[64,1024,128]{1,2,0:T(8,128)(2,1)}), bf16[64,1024,128]{1,2,0:T(8,128)(2,1)}, u32[]{:S(2)}, u32[]{:S(2)}) async-start(bf16[64,1024,128]{1,2,0:T(8,128)(2,1)} %stack.8), calls=%async_computation | async-start | bytes 33554432 | tf_op jit(solution)/shard_map/all_to_all | solution.py:138
  29.1 0.0 copy-start.6
  29.1 0.0 reduce-scatter.2.cloned.1.call-start
  29.2 0.0 copy-done.8
  29.2 0.8 fusion.44
  30.1 1.0 fusion.43
  31.7 0.0 copy-done.5
  31.7 0.0 copy-start.7
  31.8 0.5 copy.12
  32.3 0.3 convert.25
  32.6 0.6 fusion.41
  33.2 0.4 fusion.36
  33.6 0.1 maximum_bitcast_fusion
  33.7 0.7 copy.14
  34.4 1.5 broadcast_in_dim.135
  35.8 0.0 copy-done.6
  35.9 1.4 subtract_convert_fusion.1
  37.3 0.1 pad_maximum_fusion.1
  37.4 0.0 copy-done.7
  37.4 7.0 %conditional.2 = ((f32[1,8,512]{2,1,0:T(8,128)S(1)}, f32[1,8,512]{2,1,0:T(8,128)S(1)}, f32[1,8,512,128]{3,2,1,0:T(8,128)})) conditional(s32[]{:T(128)} %convert_element_type.95, (f32[1,8,512]{2,1,0:T(8,128)S(1)}, f32[1,8,512]{2,1,0:T(8,128)S(1)}, f32[1,8,512,128]{3,2,1,0:T(8,128)}) %tuple.39, (pred[512,512]{0,1:T(8,128)(4,1)S(1)}, ...), branch_computations={%region_1.2_spmd, %region_2.0_spmd} | conditional | flops 1102065664 | bytes 48496728 | solution.py:109
  37.4 0.0 copy-start
  37.4 1.5 fusion.2
  39.0 0.0 copy-done
  39.0 3.1 bitcast_add_fusion
  42.1 0.0 copy-start.1
  42.1 2.0 fusion.4
  44.2 0.0 copy-done.1
  44.4 0.1 pad_maximum_fusion
  44.5 103.7 %while.28 = (s32[]{:T(128)}, bf16[2,512,128]{2,1,0:T(8,128)(2,1)S(1)}, f32[1,8,512]{2,1,0:T(8,128)S(1)}, f32[1,8,512]{2,1,0:T(8,128)S(1)}, f32[1,8,512,128]{3,2,...) while((s32[]{:T(128)}, ...), condition=%wide.region_11.12_spmd.clone.clone, body=%wide.region_5.11_spmd.clone.clone.sunk | while | flops 1103378432 | bytes 50349432 | solution.py:127
  44.5 2.9 collective-permute-start
  47.5 0.8 dynamic_slice.35
  48.2 1.1 fusion.49
  50.0 49.7 %collective-permute-done = bf16[2,512,128]{2,1,0:T(8,128)(2,1)S(1)} collective-permute-done((bf16[2,512,128]{2,1,0:T(8,128)(2,1)S(1)}, bf16[2,512,128]{2,1,0:T(8,128)(2,1)S(1)}, u32[]{:S(2)}, u32[]{:S(2)}) %collective-permute-start) | collective-permute-done | bytes 262176 | tf_op jit(solution)/shard_map/while/body/eval_jaxpr/ppermute | solution.py:15
  99.7 12.6 %collective-permute-start = (bf16[2,512,128]{2,1,0:T(8,128)(2,1)S(1)}, bf16[2,512,128]{2,1,0:T(8,128)(2,1)S(1)}, u32[]{:S(2)}, u32[]{:S(2)}) collective-permute-start(bf16[2,512,128]{2,1,0:T(8,128)(2,1)S(1)} %get-tuple-element.546), channel_id=1, source_target_pairs={{0,4},{4,8},{8,12},{12,16},{16,20},{20,24},{24,28},{28,32},{32,36}... | collective-permute-start | bytes 786440 | tf_op jit(solution)/shard_map/while/body/eval_jaxpr/ppermute | solution.py:15
  112.4 0.8 dynamic_slice.35
  113.1 1.1 fusion.49
  114.9 10.4 %collective-permute-done = bf16[2,512,128]{2,1,0:T(8,128)(2,1)S(1)} collective-permute-done((bf16[2,512,128]{2,1,0:T(8,128)(2,1)S(1)}, bf16[2,512,128]{2,1,0:T(8,128)(2,1)S(1)}, u32[]{:S(2)}, u32[]{:S(2)}) %collective-permute-start) | collective-permute-done | bytes 262176 | tf_op jit(solution)/shard_map/while/body/eval_jaxpr/ppermute | solution.py:15
  125.3 4.4 collective-permute-start
  129.7 0.8 dynamic_slice.35
  130.5 1.1 fusion.49
  132.2 2.2 collective-permute-done
  134.5 10.4 %collective-permute-start = (bf16[2,512,128]{2,1,0:T(8,128)(2,1)S(1)}, bf16[2,512,128]{2,1,0:T(8,128)(2,1)S(1)}, u32[]{:S(2)}, u32[]{:S(2)}) collective-permute-start(bf16[2,512,128]{2,1,0:T(8,128)(2,1)S(1)} %get-tuple-element.546), channel_id=1, source_target_pairs={{0,4},{4,8},{8,12},{12,16},{16,20},{20,24},{24,28},{28,32},{32,36}... | collective-permute-start | bytes 786440 | tf_op jit(solution)/shard_map/while/body/eval_jaxpr/ppermute | solution.py:15
  145.0 0.8 dynamic_slice.35
  145.8 1.1 fusion.49
  147.5 0.7 collective-permute-done
  148.3 1.9 copy.15
  150.2 0.3 divide_convert_fusion
  150.5 252.9 %all-to-all-done = bf16[64,1024,128]{1,2,0:T(8,128)(2,1)} async-done(((bf16[64,1024,128]{1,2,0:T(8,128)(2,1)}), bf16[64,1024,128]{1,2,0:T(8,128)(2,1)}, u32[]{:S(2)}, u32[]{:S(2)}) %all-to-all-start) | async-done | bytes 16777248 | tf_op jit(solution)/shard_map/all_to_all | solution.py:138
  403.4 29.8 %convolution_convert_fusion = bf16[512,8192]{1,0:T(8,128)(2,1)} fusion(bf16[512,1024]{0,1:T(8,128)(2,1)S(1)} %bitcast.82, bf16[1024,8192]{0,1:T(8,128)(2,1)} %bitcast.36), kind=kOutput, calls=%fused_computation.45 | convolution fusion | flops 8594128896 | bytes 26214400 | tf_op jit(solution)/shard_map/dot_general | solution.py:135
  433.2 0.0 copy-start.4
  433.2 0.0 reduce-scatter.2.cloned.1.call-update
  433.3 152.3 %reduce-scatter.2.cloned.1.call-done = bf16[128,8192]{1,0:T(8,128)(2,1)} async-done(((bf16[512,8192]{1,0:T(8,128)(2,1)}), bf16[128,8192]{1,0:T(8,128)(2,1)}) %reduce-scatter.2.cloned.1.call-update) | async-done | bytes 2097168 | tf_op jit(solution)/shard_map/reduce_scatter | solution.py:143
  585.6 0.0 copy-done.4
  585.6 3.4 add_convert_fusion
  (31 shorter events, 0.2 us)
Async XLA Ops:
  13.6 15.6 %copy-start.8 = (s32[3,512]{1,0:T(4,128)S(1)}, s32[3,512]{1,0:T(4,128)}, u32[]{:S(2)}) copy-start(s32[3,512]{1,0:T(4,128)} %param.16) | copy-start | bytes 18436
  13.6 18.1 %copy-start.5 = (bf16[512,1024]{1,0:T(8,128)(2,1)S(1)}, bf16[512,1024]{1,0:T(8,128)(2,1)}, u32[]{:S(2)}) copy-start(bf16[512,1024]{1,0:T(8,128)(2,1)} %param.13) | copy-start | bytes 3145732
  13.6 389.8 %all-to-all-start = ((bf16[64,1024,128]{1,2,0:T(8,128)(2,1)}), bf16[64,1024,128]{1,2,0:T(8,128)(2,1)}, u32[]{:S(2)}, u32[]{:S(2)}) async-start(bf16[64,1024,128]{1,2,0:T(8,128)(2,1)} %stack.8), calls=%async_computation | async-start | bytes 33554432 | tf_op jit(solution)/shard_map/all_to_all | solution.py:138
  29.1 6.7 %copy-start.6 = (bf16[512,128]{1,0:T(8,128)(2,1)S(1)}, bf16[512,128]{1,0:T(8,128)(2,1)}, u32[]{:S(2)}) copy-start(bf16[512,128]{1,0:T(8,128)(2,1)} %param.14) | copy-start | bytes 393220
  29.1 556.5 %reduce-scatter.2.cloned.1.call-start = ((), (), s32[]{:S(2)}) async-start(), calls=%async_computation.2 | async-start | bytes 10485760 | tf_op jit(solution)/shard_map/reduce_scatter | solution.py:143
  31.7 5.6 copy-start.7
  37.4 1.6 copy-start
  42.1 2.1 copy-start.1
  44.5 55.1 %collective-permute-start = (bf16[2,512,128]{2,1,0:T(8,128)(2,1)S(1)}, bf16[2,512,128]{2,1,0:T(8,128)(2,1)S(1)}, u32[]{:S(2)}, u32[]{:S(2)}) collective-permute-start(bf16[2,512,128]{2,1,0:T(8,128)(2,1)S(1)} %get-tuple-element.546), channel_id=1, source_target_pairs={{0,4},{4,8},{8,12},{12,16},{16,20},{20,24},{24,28},{28,32},{32,36}... | collective-permute-start | bytes 786440 | tf_op jit(solution)/shard_map/while/body/eval_jaxpr/ppermute | solution.py:15
  99.7 25.5 %collective-permute-start = (bf16[2,512,128]{2,1,0:T(8,128)(2,1)S(1)}, bf16[2,512,128]{2,1,0:T(8,128)(2,1)S(1)}, u32[]{:S(2)}, u32[]{:S(2)}) collective-permute-start(bf16[2,512,128]{2,1,0:T(8,128)(2,1)S(1)} %get-tuple-element.546), channel_id=1, source_target_pairs={{0,4},{4,8},{8,12},{12,16},{16,20},{20,24},{24,28},{28,32},{32,36}... | collective-permute-start | bytes 786440 | tf_op jit(solution)/shard_map/while/body/eval_jaxpr/ppermute | solution.py:15
  125.3 9.2 %collective-permute-start = (bf16[2,512,128]{2,1,0:T(8,128)(2,1)S(1)}, bf16[2,512,128]{2,1,0:T(8,128)(2,1)S(1)}, u32[]{:S(2)}, u32[]{:S(2)}) collective-permute-start(bf16[2,512,128]{2,1,0:T(8,128)(2,1)S(1)} %get-tuple-element.546), channel_id=1, source_target_pairs={{0,4},{4,8},{8,12},{12,16},{16,20},{20,24},{24,28},{28,32},{32,36}... | collective-permute-start | bytes 786440 | tf_op jit(solution)/shard_map/while/body/eval_jaxpr/ppermute | solution.py:15
  134.5 13.7 %collective-permute-start = (bf16[2,512,128]{2,1,0:T(8,128)(2,1)S(1)}, bf16[2,512,128]{2,1,0:T(8,128)(2,1)S(1)}, u32[]{:S(2)}, u32[]{:S(2)}) collective-permute-start(bf16[2,512,128]{2,1,0:T(8,128)(2,1)S(1)} %get-tuple-element.546), channel_id=1, source_target_pairs={{0,4},{4,8},{8,12},{12,16},{16,20},{20,24},{24,28},{28,32},{32,36}... | collective-permute-start | bytes 786440 | tf_op jit(solution)/shard_map/while/body/eval_jaxpr/ppermute | solution.py:15
  433.2 152.4 %copy-start.4 = (bf16[128,8192]{1,0:T(8,128)(2,1)S(1)}, bf16[128,8192]{1,0:T(8,128)(2,1)}, u32[]{:S(2)}) copy-start(bf16[128,8192]{1,0:T(8,128)(2,1)} %param.19) | copy-start | bytes 6291460
Sparse Core Ops, SparseCore 0:
  433.4 152.1 reduce-scatter.1
